TPU v7x, 256 devices: a whole 4x4x8 slice. The times are simulated.
256 devices in a mesh: batch: 64 (over z, y, core), group: 4 (over x).
Axes of the slice: x: 4, y: 4, z: 8, core: 2. Of those that a mesh axis runs over, the one named last changes fastest.
Arguments:
- samples_in: float32 [16384, 8192], P('batch', 'group'), may hold values from -8 to 8, as said below
- second_samples_in: float32 [16384, 8192], P('batch', 'group'), may hold values from -8 to 8, as said below
Outputs:
- standard: float32 [16384, 8192], P(None, ('group', 'batch'))
- second_standard: float32 [16384, 8192], P(None, ('group', 'batch'))
Inputs may be any that keep to these rules, and one draw needn't show every extreme that they name: samples_in holds numbers from -8 to 8. second_samples_in holds numbers from -8 to 8.
All inputs are finite; a program needn't handle non-finite values.
Results may differ from a plain program's by a relative error of at most 0.0003.
Values sent between devices are 32-bit elements.
A program may use at most 64 MiB of HBM per device.

v0:
```python
import functools

import jax
import jax.numpy as jnp
from jax import lax
from jax.experimental import pallas as pl
from jax.experimental.pallas import tpu as pltpu
from jax.sharding import PartitionSpec as P

MESH = pl.DeviceIdType.MESH
LANES = 128


def loop(count, body, init):
    if count <= 8:
        for step in range(count):
            init = body(step, init)
        return init
    return lax.fori_loop(0, count, body, init)


def kernel(n, first_hbm, second_hbm, got, total, raw, turned, load_sem, send_sem, recv_sem, here):
    ins = (first_hbm, second_hbm)
    rows, width = first_hbm.shape
    block = width // n
    half, quarter = n // 2, n // 4
    span = half * block
    me = lax.axis_index("batch")

    def load(side, a):
        return pltpu.make_async_copy(
            ins[a].at[:, side * span : (side + 1) * span], raw.at[a, side], load_sem.at[a, side]
        )

    for side in range(2):
        for a in range(2):
            load(side, a).start()

    barrier = pltpu.get_barrier_semaphore()

    def greet(target, carry):
        pl.semaphore_signal(
            barrier, inc=1, device_id={"batch": target}, device_id_type=MESH
        )
        return carry

    lax.fori_loop(me + 1, n, greet, 0)

    def send(a, target):
        return pltpu.make_async_remote_copy(
            src_ref=turned.at[a, target],
            dst_ref=got.at[a, me],
            send_sem=send_sem.at[a, target],
            recv_sem=recv_sem.at[a, me],
            device_id={"batch": target},
            device_id_type=MESH,
        )

    def arrival(a, source):
        return pltpu.make_async_remote_copy(
            src_ref=turned.at[a, source],
            dst_ref=got.at[a, source],
            send_sem=send_sem.at[a, source],
            recv_sem=recv_sem.at[a, source],
            device_id={"batch": source},
            device_id_type=MESH,
        )

    def transpose(side, a):
        load(side, a).wait()
        for start in range(0, span, LANES):
            tile = raw[a, side, :, start : start + LANES].T
            spot = side * half + start // block
            turned[a, spot : spot + LANES // block] = tile.reshape(LANES // block, block, rows)

    def push(a, first):
        def one(step, carry):
            target = first + step

            @pl.when(target != me)
            def _():
                if a == 0:

                    @pl.when(target > me)
                    def _():
                        pl.semaphore_wait(here.at[target], 1)

                send(a, target).start()

            return carry

        loop(quarter, one, 0)

    transpose(0, 0)

    @pl.when(me > 0)
    def _():
        pl.semaphore_wait(barrier, me)

    def announce(target, carry):
        pl.semaphore_signal(
            here.at[me], inc=1, device_id={"batch": target}, device_id_type=MESH
        )
        return carry

    lax.fori_loop(0, me, announce, 0)
    push(0, 0)
    transpose(0, 1)
    push(1, 0)
    push(0, quarter)
    push(1, quarter)
    transpose(1, 0)
    transpose(1, 1)
    for first in (half, half + quarter):
        push(0, first)
        push(1, first)

    def add(sums, values):
        low, high = sums
        for start in range(0, rows, LANES):
            part = values[:, start : start + LANES]
            low += jnp.minimum(part, 1.0)
            high += jnp.maximum(part, 1.0)
        return low, high

    zero = jnp.zeros((block, LANES), jnp.float32)
    for a in range(2):
        got[a, me] = turned[a, me]

    def take(source, sums):
        @pl.when(source != me)
        def _():
            for a in range(2):
                arrival(a, source).wait_recv()

        return tuple(add(sums[a], got[a, source]) for a in range(2))

    sums = loop(n, take, ((zero, zero), (zero, zero)))
    for a in range(2):
        for kind in range(2):
            total[a, kind] = sums[a][kind]

    def drain(target, carry):
        @pl.when(target != me)
        def _():
            for a in range(2):
                send(a, target).wait_send()

        return carry

    loop(n, drain, 0)


def rescale(got, total, first_out, second_out, ready, store_sem):
    _, n, block, rows = got.shape
    outs = (first_out, second_out)
    pieces = min(n, 4)
    each = n // pieces
    copies = []
    for a in range(2):
        low, high = (
            jnp.sum(total[a, kind], axis=1, keepdims=True) / (n * rows) for kind in range(2)
        )
        scale = 1.0 / (high - low + 0.1)
        low = jnp.broadcast_to(low, (block, rows))
        scale = jnp.broadcast_to(scale, (block, rows))
        for piece in range(pieces):

            def turn(step, carry, a=a, piece=piece, low=low, scale=scale):
                source = piece * each + step
                start = source * rows
                if not isinstance(start, int):
                    start = pl.multiple_of(start, LANES)
                ready[a, :, pl.ds(start, rows)] = (got[a, source] - low) * scale
                return carry

            loop(each, turn, 0)
            part = pl.ds(piece * each * rows, each * rows)
            copy = pltpu.make_async_copy(
                ready.at[a, :, part], outs[a].at[:, part], store_sem.at[a, piece]
            )
            copy.start()
            copies.append(copy)
    for copy in copies:
        copy.wait()


def solution(mesh):
    n = mesh.shape["batch"]

    def shards(samples_in, second_samples_in):
        rows, width = samples_in.shape
        block = width // n
        half = n // 2
        held = 2 * rows * width * 4
        got, total = pl.pallas_call(
            functools.partial(kernel, n),
            out_shape=(
                pltpu.VMEM((2, n, block, rows), jnp.float32),
                pltpu.VMEM((2, 2, block, LANES), jnp.float32),
            ),
            in_specs=[pl.BlockSpec(memory_space=pltpu.HBM)] * 2,
            out_specs=[pl.BlockSpec(memory_space=pltpu.VMEM)] * 2,
            scratch_shapes=[
                pltpu.VMEM((2, 2, rows, half * block), jnp.float32),
                pltpu.VMEM((2, n, block, rows), jnp.float32),
                pltpu.SemaphoreType.DMA((2, 2)),
                pltpu.SemaphoreType.DMA((2, n)),
                pltpu.SemaphoreType.DMA((2, n)),
                pltpu.SemaphoreType.REGULAR((n,)),
            ],
            compiler_params=pltpu.CompilerParams(
                collective_id=0, has_side_effects=True, vmem_limit_bytes=4 * held + (8 << 20)
            ),
            name="exchange",
        )(
            pltpu.with_memory_space_constraint(samples_in, pltpu.HBM),
            pltpu.with_memory_space_constraint(second_samples_in, pltpu.HBM),
        )
        out = jax.ShapeDtypeStruct((block, n * rows), jnp.float32)
        first, second = pl.pallas_call(
            rescale,
            out_shape=(out, out),
            in_specs=[pl.BlockSpec(memory_space=pltpu.VMEM)] * 2,
            out_specs=[pl.BlockSpec(memory_space=pl.ANY)] * 2,
            scratch_shapes=[
                pltpu.VMEM((2, block, n * rows), jnp.float32),
                pltpu.SemaphoreType.DMA((2, min(n, 4))),
            ],
            compiler_params=pltpu.CompilerParams(vmem_limit_bytes=2 * held + (8 << 20)),
            name="rescale",
        )(
            pltpu.with_memory_space_constraint(got, pltpu.VMEM),
            pltpu.with_memory_space_constraint(total, pltpu.VMEM),
        )
        return first.T, second.T

    placed = (P("batch", "group"), P("batch", "group"))
    return jax.shard_map(
        shards,
        mesh=mesh,
        in_specs=placed,
        out_specs=(P(None, ("group", "batch")), P(None, ("group", "batch"))),
        check_vma=False,
    )
```

profile of v0, /device:TPU:224, one launch (start us, length us, event | category | flops | bytes accessed | tf_op | source)
XLA Modules:
  0.0 110.4 jit_solution(1655720560384190479)
XLA Ops:
  0.6 107.5 %exchange.1 = (f32[2,64,32,256]{3,2,1,0:T(8,128)S(1)}, f32[2,2,32,128]{3,2,1,0:T(8,128)S(1)}) custom-call(f32[256,2048]{1,0:T(8,128)} %first_hbm.1, f32[256,2048]{1,0:T(8,128)} %second_hbm.1), custom_call_target="tpu_custom_call" | custom-call | tf_op jit(solution)/shard_map/exchange/pallas_call | solution.py:196
  108.2 2.3 %rescale.1 = (f32[32,16384]{1,0:T(8,128)}, f32[32,16384]{1,0:T(8,128)}) custom-call(f32[2,64,32,256]{3,2,1,0:T(8,128)S(1)} %get-tuple-element.6.got, f32[2,2,32,128]{3,2,1,0:T(8,128)S(1)} %get-tuple-element.7.total), custom_call_target="tpu_custom_call" | custom-call | tf_op jit(solution)/shard_map/rescale/pallas_call | solution.py:221
where the time goes:
time: 112 us; the launch traced here: 110 us
  Pallas kernels  110 us (98%)
    pallas_call x1, Pallas kernels, shards(): pl.pallas_call(functools.partial(kernel, n), out_shape=(pltpu.VMEM((2, n,...  108 us
    pallas_call x1, Pallas kernels, shards(): pl.pallas_call(rescale, out_shape=(out, out), in_specs=[pl.BlockSpec(memo...  2.26 us

commit v1 on v0

v1 whole, which is shorter than its diff:
```python
import functools

import jax
import jax.numpy as jnp
from jax import lax
from jax.experimental import pallas as pl
from jax.experimental.pallas import tpu as pltpu
from jax.sharding import PartitionSpec as P

MESH = pl.DeviceIdType.MESH
LANES = 128
PLANES = 8
PER = 8
HALF = 4


def kernel(first_hbm, second_hbm, got, total, raw, turned, load_sem, send_sem, recv_sem, here, open_sem):
    n = PLANES * PER
    ins = (first_hbm, second_hbm)
    rows, width = first_hbm.shape
    block = width // n
    chunk = PER * block
    near = HALF * PER
    me = lax.axis_index("batch")
    z, y, c = me // PER, (me % PER) // 2, me % 2
    early = z < HALF

    def plane(k):
        return (z + k) % HALF + HALF * (k // HALF)

    def load(k, a):
        start = pl.multiple_of(plane(k) * chunk, chunk)
        return pltpu.make_async_copy(ins[a].at[:, pl.ds(start, chunk)], raw.at[k, a], load_sem.at[k, a])

    for k in range(PLANES):
        for a in range(2):
            load(k, a).start()

    barrier = pltpu.get_barrier_semaphore()

    def greet(target, carry):
        @pl.when(target != me)
        def _():
            pl.semaphore_signal(barrier, inc=1, device_id={"batch": target}, device_id_type=MESH)

        return carry

    @pl.when(early)
    def _():
        lax.fori_loop(0, n, greet, 0)

    def announce(target, carry):
        pl.semaphore_signal(here.at[me], inc=1, device_id={"batch": target}, device_id_type=MESH)
        return carry

    @pl.when(jnp.logical_not(early))
    def _():
        pl.semaphore_wait(barrier, near)
        lax.fori_loop(0, near, announce, 0)

    def transpose(k):
        for a in range(2):
            load(k, a).wait()
            for start in range(0, chunk, LANES):
                tile = raw[k, a, :, start : start + LANES].T
                spot = start // block
                turned[k, spot : spot + LANES // block, a] = tile.reshape(LANES // block, block, rows)

    def send(k, q, target):
        return pltpu.make_async_remote_copy(
            src_ref=turned.at[k, q],
            dst_ref=got.at[me],
            send_sem=send_sem.at[target],
            recv_sem=recv_sem.at[me],
            device_id={"batch": target},
            device_id_type=MESH,
        )

    def spot(step, first):
        k = first + step % HALF
        turn = step // HALF
        q = (y + turn // 2 + k + 2 * c) % 4 * 2 + (c + turn) % 2
        return k, q, plane(k) * PER + q

    def push_early(step, carry):
        k, q, target = spot(step, 0)

        @pl.when(target != me)
        def _():
            send(k, q, target).start()

        return carry

    def push_late(step, carry):
        k, q, target = spot(step, HALF)

        @pl.when(target != me)
        def _():
            @pl.when(early)
            def _():
                pl.semaphore_wait(here.at[target], 1)

            send(k, q, target).start()

        return carry

    for k in range(HALF):
        transpose(k)

    @pl.when(early)
    def _():
        pl.semaphore_wait(barrier, near - 1)

    lax.fori_loop(0, near, push_early, 0)
    for k in range(HALF, PLANES):
        transpose(k)

    @pl.when(jnp.logical_not(early))
    def _():
        pl.semaphore_wait(open_sem, 1)

    lax.fori_loop(0, near, push_late, 0)

    @pl.when(early)
    def _():
        pl.semaphore_signal(
            open_sem, inc=1, device_id={"batch": (PLANES - 1 - z) * PER + me % PER}, device_id_type=MESH
        )

    own = z // HALF * HALF
    got[me] = turned[own, me % PER]

    def add(sums, values):
        low, high = sums
        for start in range(0, rows, LANES):
            part = values[:, start : start + LANES]
            low += jnp.minimum(part, 1.0)
            high += jnp.maximum(part, 1.0)
        return low, high

    def take(source, sums):
        @pl.when(source != me)
        def _():
            pltpu.make_async_remote_copy(
                src_ref=turned.at[0, 0],
                dst_ref=got.at[source],
                send_sem=send_sem.at[source],
                recv_sem=recv_sem.at[source],
                device_id={"batch": source},
                device_id_type=MESH,
            ).wait_recv()

        return tuple(add(sums[a], got[source, a]) for a in range(2))

    zero = jnp.zeros((block, LANES), jnp.float32)
    sums = lax.fori_loop(0, n, take, ((zero, zero), (zero, zero)))
    for a in range(2):
        for kind in range(2):
            total[a, kind] = sums[a][kind]

    def drain(step, carry):
        k, q, target = spot(step % near, step // near * HALF)

        @pl.when(target != me)
        def _():
            send(k, q, target).wait_send()

        return carry

    lax.fori_loop(0, n, drain, 0)


def rescale(got, total, first_out, second_out, ready, store_sem):
    n, _, block, rows = got.shape
    outs = (first_out, second_out)
    pieces = 4
    each = n // pieces
    copies = []
    for a in range(2):
        low, high = (
            jnp.sum(total[a, kind], axis=1, keepdims=True) / (n * rows) for kind in range(2)
        )
        scale = 1.0 / (high - low + 0.1)
        low = jnp.broadcast_to(low, (block, rows))
        scale = jnp.broadcast_to(scale, (block, rows))
        for piece in range(pieces):

            def turn(step, carry, a=a, piece=piece, low=low, scale=scale):
                source = piece * each + step
                start = pl.multiple_of(source * rows, LANES)
                ready[a, :, pl.ds(start, rows)] = (got[source, a] - low) * scale
                return carry

            lax.fori_loop(0, each, turn, 0)
            part = pl.ds(piece * each * rows, each * rows)
            copy = pltpu.make_async_copy(
                ready.at[a, :, part], outs[a].at[:, part], store_sem.at[a, piece]
            )
            copy.start()
            copies.append(copy)
    for copy in copies:
        copy.wait()


def solution(mesh):
    n = mesh.shape["batch"]

    def shards(samples_in, second_samples_in):
        rows, width = samples_in.shape
        block = width // n
        held = 2 * rows * width * 4
        got, total = pl.pallas_call(
            kernel,
            out_shape=(
                pltpu.VMEM((n, 2, block, rows), jnp.float32),
                pltpu.VMEM((2, 2, block, LANES), jnp.float32),
            ),
            in_specs=[pl.BlockSpec(memory_space=pltpu.HBM)] * 2,
            out_specs=[pl.BlockSpec(memory_space=pltpu.VMEM)] * 2,
            scratch_shapes=[
                pltpu.VMEM((PLANES, 2, rows, PER * block), jnp.float32),
                pltpu.VMEM((PLANES, PER, 2, block, rows), jnp.float32),
                pltpu.SemaphoreType.DMA((PLANES, 2)),
                pltpu.SemaphoreType.DMA((n,)),
                pltpu.SemaphoreType.DMA((n,)),
                pltpu.SemaphoreType.REGULAR((n,)),
                pltpu.SemaphoreType.REGULAR,
            ],
            compiler_params=pltpu.CompilerParams(
                collective_id=0, has_side_effects=True, vmem_limit_bytes=4 * held + (8 << 20)
            ),
            name="exchange",
        )(
            pltpu.with_memory_space_constraint(samples_in, pltpu.HBM),
            pltpu.with_memory_space_constraint(second_samples_in, pltpu.HBM),
        )
        out = jax.ShapeDtypeStruct((block, n * rows), jnp.float32)
        first, second = pl.pallas_call(
            rescale,
            out_shape=(out, out),
            in_specs=[pl.BlockSpec(memory_space=pltpu.VMEM)] * 2,
            out_specs=[pl.BlockSpec(memory_space=pl.ANY)] * 2,
            scratch_shapes=[
                pltpu.VMEM((2, block, n * rows), jnp.float32),
                pltpu.SemaphoreType.DMA((2, 4)),
            ],
            compiler_params=pltpu.CompilerParams(vmem_limit_bytes=2 * held + (8 << 20)),
            name="rescale",
        )(
            pltpu.with_memory_space_constraint(got, pltpu.VMEM),
            pltpu.with_memory_space_constraint(total, pltpu.VMEM),
        )
        return first.T, second.T

    placed = (P("batch", "group"), P("batch", "group"))
    return jax.shard_map(
        shards,
        mesh=mesh,
        in_specs=placed,
        out_specs=(P(None, ("group", "batch")), P(None, ("group", "batch"))),
        check_vma=False,
    )
```

time: 112 us -> 111 us (level)
    pallas_call x1, Pallas kernels: 108 us -> 106 us  [shards(): pl.pallas_call(kernel, out_shape=(pltpu.VMEM((n, 2, block, rows), jnp.flo...]
where the time goes in v1:
time: 111 us; the launch traced here: 109 us
  Pallas kernels  109 us (98%)
    pallas_call x1, Pallas kernels, shards(): pl.pallas_call(kernel, out_shape=(pltpu.VMEM((n, 2, block, rows), jnp.flo...  106 us
    pallas_call x1, Pallas kernels, shards(): pl.pallas_call(rescale, out_shape=(out, out), in_specs=[pl.BlockSpec(memo...  2.26 us

profile of v1, /device:TPU:224, one launch (start us, length us, event | category | flops | bytes accessed | tf_op | source)
XLA Modules:
  0.0 109.3 jit_solution(17004479919925848786)
XLA Ops:
  0.6 106.4 %exchange.1 = (f32[64,2,32,256]{3,2,1,0:T(8,128)S(1)}, f32[2,2,32,128]{3,2,1,0:T(8,128)S(1)}) custom-call(f32[256,2048]{1,0:T(8,128)} %first_hbm.1, f32[256,2048]{1,0:T(8,128)} %second_hbm.1), custom_call_target="tpu_custom_call" | custom-call | tf_op jit(solution)/shard_map/exchange/pallas_call | solution.py:212
  107.0 2.3 %rescale.1 = (f32[32,16384]{1,0:T(8,128)}, f32[32,16384]{1,0:T(8,128)}) custom-call(f32[64,2,32,256]{3,2,1,0:T(8,128)S(1)} %get-tuple-element.6.got, f32[2,2,32,128]{3,2,1,0:T(8,128)S(1)} %get-tuple-element.7.total), custom_call_target="tpu_custom_call" | custom-call | tf_op jit(solution)/shard_map/rescale/pallas_call | solution.py:238

commit v2 on v1

v2 whole, which is shorter than its diff:
```python
import functools

import jax
import jax.numpy as jnp
from jax import lax
from jax.experimental import pallas as pl
from jax.experimental.pallas import tpu as pltpu
from jax.sharding import PartitionSpec as P

MESH = pl.DeviceIdType.MESH
LANES = 128
PLANES = 8
PER = 8
ORDER = (4, 3, 5, 2, 6, 1, 7, 0)
SHIFT = (0, 0, 1, 0, 1, 0, 1, 0)
LOADS = (1, 7, 4, 3, 5, 2, 6, 0)
FIRST = 3
PHASES = (('F', 0, 3), ('A', 3, 8))
STEPS = sum(d * 8**i for i, d in enumerate(ORDER))
TURNS = sum(d * 4**i for i, d in enumerate(SHIFT))
NEAR = sum((d in (1, PLANES - 1)) << i for i, d in enumerate(ORDER))
OWN = ORDER.index(0)


def at(table, bits, i):
    return lax.shift_right_logical(jnp.int32(table), bits * i) % 2**bits


def kernel(first_hbm, second_hbm, got, total, raw, turned, load_sem, send_sem, recv_sem, here):
    n = PLANES * PER
    ins = (first_hbm, second_hbm)
    rows, width = first_hbm.shape
    block = width // n
    chunk = PER * block
    me = lax.axis_index("batch")
    z, y, c = me // PER, (me % PER) // 2, me % 2

    def plane(k):
        return (z + LOADS[k]) % PLANES

    for k in range(PLANES):
        for a in range(2):
            start = pl.multiple_of(plane(k) * chunk, chunk)
            pltpu.make_async_copy(
                ins[a].at[:, pl.ds(start, chunk)], raw.at[k, a], load_sem.at[k]
            ).start()

    barrier = pltpu.get_barrier_semaphore()

    def greet(step, carry):
        side = step // PER * (PLANES - 2) + 1
        target = (z + side) % PLANES * PER + (me + step) % PER
        pl.semaphore_signal(barrier, inc=1, device_id={"batch": target}, device_id_type=MESH)
        return carry

    lax.fori_loop(0, 2 * PER, greet, 0)

    def hail(which, dz):
        for slot, d in ((0, dz), (1, PLANES - dz)):
            target = (z + d) % PLANES * PER + me % PER
            pl.semaphore_signal(
                here.at[which, slot], inc=1, device_id={"batch": target}, device_id_type=MESH
            )

    def heard(which):
        for slot in range(2):
            pl.semaphore_wait(here.at[which, slot], 1)

    def transpose(k):
        pltpu.make_async_copy(raw.at[k], raw.at[k], load_sem.at[k]).wait()
        for a in range(2):
            for start in range(0, chunk, LANES):
                tile = raw[k, a, :, start : start + LANES].T
                spot = plane(k) * PER + start // block
                turned[pl.ds(spot, LANES // block), a] = tile.reshape(LANES // block, block, rows)

    def push(mask, r0, r1):
        def one(step, carry):
            i = step % PLANES
            turn = step // PLANES
            zt = (z + at(STEPS, 3, i)) % PLANES
            target = zt * PER + (y + turn // 2 + at(TURNS, 2, i) + 2 * c) % 4 * 2 + (c + turn) % 2
            ok = target != me
            if mask != "A":
                ok = ok & (at(NEAR, 1, i) == (1 if mask == "N" else 0))

            @pl.when(ok)
            def _():
                pltpu.make_async_remote_copy(
                    src_ref=turned.at[target],
                    dst_ref=got.at[me],
                    send_sem=send_sem,
                    recv_sem=recv_sem.at[turn],
                    device_id={"batch": target},
                    device_id_type=MESH,
                ).start()

            return carry

        lax.fori_loop(r0 * PLANES, r1 * PLANES, one, 0)

    for k in range(2):
        transpose(k)
    pl.semaphore_wait(barrier, 2 * PER)
    hail(0, 1)
    push("N", 0, FIRST)
    for k in range(2, 5):
        transpose(k)
    heard(0)
    hail(1, 2)
    for k in range(5, PLANES):
        transpose(k)
    heard(1)
    for mask, r0, r1 in PHASES:
        push(mask, r0, r1)

    got[me] = turned[me]

    def arrived(count, turn):
        pieces = pl.ds(0, count)
        pltpu.make_async_remote_copy(
            src_ref=turned.at[pieces],
            dst_ref=got.at[pieces],
            send_sem=send_sem,
            recv_sem=recv_sem.at[turn],
            device_id={"batch": (me + 1) % n},
            device_id_type=MESH,
        ).wait_recv()

    def take(turn, sums):
        own = turn == (8 - SHIFT[OWN] - 2 * c) % 4 * 2

        @pl.when(own)
        def _():
            arrived(PLANES - 1, turn)

        @pl.when(jnp.logical_not(own))
        def _():
            arrived(PLANES, turn)

        def add(i, sums):
            cs = (c + turn) % 2
            ys = (y - turn // 2 - at(TURNS, 2, i) - 2 * cs + 16) % 4
            source = (z - at(STEPS, 3, i) + PLANES) % PLANES * PER + ys * 2 + cs
            out = []
            for a in range(2):
                low, high = sums[a]
                values = got[source, a]
                for start in range(0, rows, LANES):
                    part = values[:, start : start + LANES]
                    low += jnp.minimum(part, 1.0)
                    high += jnp.maximum(part, 1.0)
                out.append((low, high))
            return tuple(out)

        return lax.fori_loop(0, PLANES, add, sums)

    zero = jnp.zeros((block, LANES), jnp.float32)
    sums = lax.fori_loop(0, PER, take, ((zero, zero), (zero, zero)))
    for a in range(2):
        for kind in range(2):
            total[a, kind] = sums[a][kind]

    others = pl.ds(0, n - 1)
    pltpu.make_async_remote_copy(
        src_ref=turned.at[others],
        dst_ref=got.at[others],
        send_sem=send_sem,
        recv_sem=recv_sem.at[0],
        device_id={"batch": (me + 1) % n},
        device_id_type=MESH,
    ).wait_send()


def rescale(got, total, first_out, second_out, ready, store_sem):
    n, _, block, rows = got.shape
    outs = (first_out, second_out)
    pieces = 4
    each = n // pieces
    copies = []
    for a in range(2):
        low, high = (
            jnp.sum(total[a, kind], axis=1, keepdims=True) / (n * rows) for kind in range(2)
        )
        scale = 1.0 / (high - low + 0.1)
        low = jnp.broadcast_to(low, (block, rows))
        scale = jnp.broadcast_to(scale, (block, rows))
        for piece in range(pieces):

            def turn(step, carry, a=a, piece=piece, low=low, scale=scale):
                source = piece * each + step
                start = pl.multiple_of(source * rows, LANES)
                ready[a, :, pl.ds(start, rows)] = (got[source, a] - low) * scale
                return carry

            lax.fori_loop(0, each, turn, 0, unroll=4)
            part = pl.ds(piece * each * rows, each * rows)
            copy = pltpu.make_async_copy(
                ready.at[a, :, part], outs[a].at[:, part], store_sem.at[a, piece]
            )
            copy.start()
            copies.append(copy)
    for copy in copies:
        copy.wait()


def solution(mesh):
    n = mesh.shape["batch"]

    def shards(samples_in, second_samples_in):
        rows, width = samples_in.shape
        block = width // n
        held = 2 * rows * width * 4
        got, total = pl.pallas_call(
            kernel,
            out_shape=(
                pltpu.VMEM((n, 2, block, rows), jnp.float32),
                pltpu.VMEM((2, 2, block, LANES), jnp.float32),
            ),
            in_specs=[pl.BlockSpec(memory_space=pltpu.HBM)] * 2,
            out_specs=[pl.BlockSpec(memory_space=pltpu.VMEM)] * 2,
            scratch_shapes=[
                pltpu.VMEM((PLANES, 2, rows, PER * block), jnp.float32),
                pltpu.VMEM((n, 2, block, rows), jnp.float32),
                pltpu.SemaphoreType.DMA((PLANES,)),
                pltpu.SemaphoreType.DMA,
                pltpu.SemaphoreType.DMA((PER,)),
                pltpu.SemaphoreType.REGULAR((2, 2)),
            ],
            compiler_params=pltpu.CompilerParams(
                collective_id=0, has_side_effects=True, vmem_limit_bytes=4 * held + (8 << 20)
            ),
            name="exchange",
        )(
            pltpu.with_memory_space_constraint(samples_in, pltpu.HBM),
            pltpu.with_memory_space_constraint(second_samples_in, pltpu.HBM),
        )
        out = jax.ShapeDtypeStruct((block, n * rows), jnp.float32)
        first, second = pl.pallas_call(
            rescale,
            out_shape=(out, out),
            in_specs=[pl.BlockSpec(memory_space=pltpu.VMEM)] * 2,
            out_specs=[pl.BlockSpec(memory_space=pl.ANY)] * 2,
            scratch_shapes=[
                pltpu.VMEM((2, block, n * rows), jnp.float32),
                pltpu.SemaphoreType.DMA((2, 4)),
            ],
            compiler_params=pltpu.CompilerParams(vmem_limit_bytes=2 * held + (8 << 20)),
            name="rescale",
        )(
            pltpu.with_memory_space_constraint(got, pltpu.VMEM),
            pltpu.with_memory_space_constraint(total, pltpu.VMEM),
        )
        return first.T, second.T

    placed = (P("batch", "group"), P("batch", "group"))
    return jax.shard_map(
        shards,
        mesh=mesh,
        in_specs=placed,
        out_specs=(P(None, ("group", "batch")), P(None, ("group", "batch"))),
        check_vma=False,
    )
```

time: 111 us -> 105 us (0.946)
  the two profiles are of different devices: /device:TPU:224 before, /device:TPU:1 now
where the time goes in v2:
time: 105 us
  Pallas kernels  104 us (99%)
    pallas_call x1, Pallas kernels, shards(): pl.pallas_call(kernel, out_shape=(pltpu.VMEM((n, 2, block, rows), jnp.flo...  102 us
    pallas_call x1, Pallas kernels, shards(): pl.pallas_call(rescale, out_shape=(out, out), in_specs=[pl.BlockSpec(memo...  2.21 us

profile of v2, /device:TPU:1, one launch (start us, length us, event | category | flops | bytes accessed | tf_op | source)
XLA Modules:
  0.0 104.8 jit_solution(1076534572314797301)
XLA Ops:
  0.6 102.0 %exchange.1 = (f32[64,2,32,256]{3,2,1,0:T(8,128)S(1)}, f32[2,2,32,128]{3,2,1,0:T(8,128)S(1)}) custom-call(f32[256,2048]{1,0:T(8,128)} %first_hbm.1, f32[256,2048]{1,0:T(8,128)} %second_hbm.1), custom_call_target="tpu_custom_call" | custom-call | tf_op jit(solution)/shard_map/exchange/pallas_call | solution.py:214
  102.6 2.2 %rescale.1 = (f32[32,16384]{1,0:T(8,128)}, f32[32,16384]{1,0:T(8,128)}) custom-call(f32[64,2,32,256]{3,2,1,0:T(8,128)S(1)} %get-tuple-element.6.got, f32[2,2,32,128]{3,2,1,0:T(8,128)S(1)} %get-tuple-element.7.total), custom_call_target="tpu_custom_call" | custom-call | tf_op jit(solution)/shard_map/rescale/pallas_call | solution.py:239

commit v3 on v2

--- a/solution.py
+++ b/solution.py
@@ -14,16 +14,22 @@
 ORDER = (4, 3, 5, 2, 6, 1, 7, 0)
 SHIFT = (0, 0, 1, 0, 1, 0, 1, 0)
 LOADS = (1, 7, 4, 3, 5, 2, 6, 0)
-FIRST = 3
-PHASES = (('F', 0, 3), ('A', 3, 8))
-STEPS = sum(d * 8**i for i, d in enumerate(ORDER))
-TURNS = sum(d * 4**i for i, d in enumerate(SHIFT))
-NEAR = sum((d in (1, PLANES - 1)) << i for i, d in enumerate(ORDER))
+FIRST = 4
+PHASES = (('F', 0, 4), ('A', 4, 6), ('O', 6, 8), ('L', 6, 8), ('H', 6, 8))
+EARLY = 4
+NEAR = (1, PLANES - 1)
 OWN = ORDER.index(0)
-
-
-def at(table, bits, i):
-    return lax.shift_right_logical(jnp.int32(table), bits * i) % 2**bits
+BESIDE = ((1, 2, 3), (3, 1, 2), (2, 3, 1), (1, 3, 2))
+
+
+def along(i, turn, core):
+    j = turn // 2
+    if ORDER[i] not in NEAR:
+        return (j + SHIFT[i] + 2 * core) % 4
+    one, two = (
+        sum(d * 4 ** (k + 1) for k, d in enumerate(BESIDE[NEAR.index(ORDER[i]) * 2 + side])) for side in range(2)
+    )
+    return lax.shift_right_logical(jnp.where(core == 0, one, two), 2 * j) % 4
 
 
 def kernel(first_hbm, second_hbm, got, total, raw, turned, load_sem, send_sem, recv_sem, here):
@@ -38,32 +44,38 @@
     def plane(k):
         return (z + LOADS[k]) % PLANES
 
-    for k in range(PLANES):
+    def load(k):
         for a in range(2):
             start = pl.multiple_of(plane(k) * chunk, chunk)
             pltpu.make_async_copy(
                 ins[a].at[:, pl.ds(start, chunk)], raw.at[k, a], load_sem.at[k]
             ).start()
 
+    for k in range(2):
+        load(k)
+
     barrier = pltpu.get_barrier_semaphore()
 
-    def greet(step, carry):
-        side = step // PER * (PLANES - 2) + 1
-        target = (z + side) % PLANES * PER + (me + step) % PER
-        pl.semaphore_signal(barrier, inc=1, device_id={"batch": target}, device_id_type=MESH)
-        return carry
-
-    lax.fori_loop(0, 2 * PER, greet, 0)
+    def device(dz, dy, dc=0):
+        return (z + dz) % PLANES * PER + (y + dy) % 4 * 2 + (c + dc) % 2
+
+    def signal(sem, target):
+        pl.semaphore_signal(sem, inc=1, device_id={"batch": target}, device_id_type=MESH)
+
+    for dz in (1, PLANES - 1):
+        for dc in range(2):
+            signal(barrier, device(dz, 0, dc))
+    for dy in range(1, 4):
+        signal(barrier, device(0, dy))
+    for k in range(2, PLANES):
+        load(k)
 
     def hail(which, dz):
         for slot, d in ((0, dz), (1, PLANES - dz)):
-            target = (z + d) % PLANES * PER + me % PER
-            pl.semaphore_signal(
-                here.at[which, slot], inc=1, device_id={"batch": target}, device_id_type=MESH
-            )
-
-    def heard(which):
-        for slot in range(2):
+            signal(here.at[which, slot], device(d, 0))
+
+    def heard(which, slots):
+        for slot in range(slots):
             pl.semaphore_wait(here.at[which, slot], 1)
 
     def transpose(k):
@@ -74,43 +86,73 @@
                 spot = plane(k) * PER + start // block
                 turned[pl.ds(spot, LANES // block), a] = tile.reshape(LANES // block, block, rows)
 
+    def send(i, turn, wanted=None):
+        zt = (z + ORDER[i]) % PLANES
+        yt = (y + along(i, turn, c)) % 4
+        target = zt * PER + yt * 2 + (c + turn) % 2
+
+        def go():
+            pltpu.make_async_remote_copy(
+                src_ref=turned.at[target],
+                dst_ref=got.at[me],
+                send_sem=send_sem,
+                recv_sem=recv_sem.at[turn],
+                device_id={"batch": target},
+                device_id_type=MESH,
+            ).start()
+
+        ok = wanted(zt, yt) if wanted else None
+        if ORDER[i] == 0:
+            ok = target != me if ok is None else ok & (target != me)
+        if ok is None:
+            go()
+        else:
+            pl.when(ok)(go)
+
+    WANTED = {
+        "O": lambda zt, yt: (zt == 0),
+        "L": lambda zt, yt: (zt < EARLY) & jnp.logical_not((zt == 0)),
+        "l": lambda zt, yt: zt < EARLY,
+        "H": lambda zt, yt: zt >= EARLY,
+    }
+
     def push(mask, r0, r1):
-        def one(step, carry):
-            i = step % PLANES
-            turn = step // PLANES
-            zt = (z + at(STEPS, 3, i)) % PLANES
-            target = zt * PER + (y + turn // 2 + at(TURNS, 2, i) + 2 * c) % 4 * 2 + (c + turn) % 2
-            ok = target != me
-            if mask != "A":
-                ok = ok & (at(NEAR, 1, i) == (1 if mask == "N" else 0))
-
-            @pl.when(ok)
-            def _():
-                pltpu.make_async_remote_copy(
-                    src_ref=turned.at[target],
-                    dst_ref=got.at[me],
-                    send_sem=send_sem,
-                    recv_sem=recv_sem.at[turn],
-                    device_id={"batch": target},
-                    device_id_type=MESH,
-                ).start()
-
+        which = [i for i in range(PLANES) if not (mask == "N" and ORDER[i] not in NEAR or mask == "F" and ORDER[i] in NEAR)]
+
+        def one(turn, carry):
+            for i in which:
+                send(i, turn, WANTED.get(mask))
             return carry
 
-        lax.fori_loop(r0 * PLANES, r1 * PLANES, one, 0)
-
-    for k in range(2):
+        if r1 - r0 <= 2 and mask in "N":
+            for turn in range(r0, r1):
+                one(turn, 0)
+        else:
+            lax.fori_loop(r0, r1, one, 0)
+
+    def pair(dz):
+        for turn in range(2):
+            send(ORDER.index(dz), turn)
+
+    transpose(0)
+    pl.semaphore_wait(barrier, 7)
+    for dy in range(1, 4):
+        signal(here.at[0, dy - 1], device(0, dy))
+    pair(1)
+    transpose(1)
+    pair(PLANES - 1)
+    for k in range(2, 4):
         transpose(k)
-    pl.semaphore_wait(barrier, 2 * PER)
-    hail(0, 1)
-    push("N", 0, FIRST)
-    for k in range(2, 5):
+    heard(0, 3)
+    hail(1, 1)
+    push("N", 2, FIRST)
+    for k in range(4, 6):
         transpose(k)
-    heard(0)
-    hail(1, 2)
-    for k in range(5, PLANES):
+    heard(1, 2)
+    hail(2, 2)
+    for k in range(6, PLANES):
         transpose(k)
-    heard(1)
+    heard(2, 2)
     for mask, r0, r1 in PHASES:
         push(mask, r0, r1)
 
@@ -138,10 +180,10 @@
         def _():
             arrived(PLANES, turn)
 
-        def add(i, sums):
+        for i in range(PLANES):
             cs = (c + turn) % 2
-            ys = (y - turn // 2 - at(TURNS, 2, i) - 2 * cs + 16) % 4
-            source = (z - at(STEPS, 3, i) + PLANES) % PLANES * PER + ys * 2 + cs
+            ys = (y - along(i, turn, cs) + 4) % 4
+            source = (z - ORDER[i] + PLANES) % PLANES * PER + ys * 2 + cs
             out = []
             for a in range(2):
                 low, high = sums[a]
@@ -151,9 +193,8 @@
                     low += jnp.minimum(part, 1.0)
                     high += jnp.maximum(part, 1.0)
                 out.append((low, high))
-            return tuple(out)
-
-        return lax.fori_loop(0, PLANES, add, sums)
+            sums = tuple(out)
+        return sums
 
     zero = jnp.zeros((block, LANES), jnp.float32)
     sums = lax.fori_loop(0, PER, take, ((zero, zero), (zero, zero)))
@@ -225,7 +266,7 @@
                 pltpu.SemaphoreType.DMA((PLANES,)),
                 pltpu.SemaphoreType.DMA,
                 pltpu.SemaphoreType.DMA((PER,)),
-                pltpu.SemaphoreType.REGULAR((2, 2)),
+                pltpu.SemaphoreType.REGULAR((3, 3)),
             ],
             compiler_params=pltpu.CompilerParams(
                 collective_id=0, has_side_effects=True, vmem_limit_bytes=4 * held + (8 << 20)

time: 105 us -> 102 us (0.971)
  the two profiles are of different devices: /device:TPU:1 before, /device:TPU:224 now
where the time goes in v3:
time: 102 us
  Pallas kernels  101 us (99%)
    pallas_call x1, Pallas kernels, shards(): pl.pallas_call(kernel, out_shape=(pltpu.VMEM((n, 2, block, rows), jnp.flo...  99.3 us
    pallas_call x1, Pallas kernels, shards(): pl.pallas_call(rescale, out_shape=(out, out), in_specs=[pl.BlockSpec(memo...  2.21 us

profile of v3, /device:TPU:224, one launch (start us, length us, event | category | flops | bytes accessed | tf_op | source)
XLA Modules:
  0.0 102.1 jit_solution(4740935661504767531)
XLA Ops:
  0.6 99.3 %exchange.1 = (f32[64,2,32,256]{3,2,1,0:T(8,128)S(1)}, f32[2,2,32,128]{3,2,1,0:T(8,128)S(1)}) custom-call(f32[256,2048]{1,0:T(8,128)} %first_hbm.1, f32[256,2048]{1,0:T(8,128)} %second_hbm.1), custom_call_target="tpu_custom_call" | custom-call | tf_op jit(solution)/shard_map/exchange/pallas_call | solution.py:255
  99.9 2.2 %rescale.1 = (f32[32,16384]{1,0:T(8,128)}, f32[32,16384]{1,0:T(8,128)}) custom-call(f32[64,2,32,256]{3,2,1,0:T(8,128)S(1)} %get-tuple-element.6.got, f32[2,2,32,128]{3,2,1,0:T(8,128)S(1)} %get-tuple-element.7.total), custom_call_target="tpu_custom_call" | custom-call | tf_op jit(solution)/shard_map/rescale/pallas_call | solution.py:280

commit v4 on v3

--- a/solution.py
+++ b/solution.py
@@ -11,11 +11,11 @@
 LANES = 128
 PLANES = 8
 PER = 8
-ORDER = (4, 3, 5, 2, 6, 1, 7, 0)
-SHIFT = (0, 0, 1, 0, 1, 0, 1, 0)
+ORDER = (7, 3, 5, 2, 6, 1, 4, 0)
+SHIFT = (1, 0, 1, 0, 1, 0, 0, 0)
 LOADS = (1, 7, 4, 3, 5, 2, 6, 0)
 FIRST = 4
-PHASES = (('F', 0, 4), ('A', 4, 6), ('O', 6, 8), ('L', 6, 8), ('H', 6, 8))
+PHASES = (('F', 0, 4), ('A', 4, 7), ('0', 7, 8), ('1', 7, 8), ('2', 7, 8), ('3', 7, 8), ('4', 7, 8))
 EARLY = 4
 NEAR = (1, PLANES - 1)
 OWN = ORDER.index(0)
@@ -109,19 +109,19 @@
         else:
             pl.when(ok)(go)
 
-    WANTED = {
-        "O": lambda zt, yt: (zt == 0),
-        "L": lambda zt, yt: (zt < EARLY) & jnp.logical_not((zt == 0)),
-        "l": lambda zt, yt: zt < EARLY,
-        "H": lambda zt, yt: zt >= EARLY,
-    }
+    def urgency(level):
+        def wanted(zt, yt):
+            first = jnp.minimum(z, zt)
+            return first >= level if level == EARLY else first == level
+
+        return wanted
 
     def push(mask, r0, r1):
         which = [i for i in range(PLANES) if not (mask == "N" and ORDER[i] not in NEAR or mask == "F" and ORDER[i] in NEAR)]
 
         def one(turn, carry):
             for i in which:
-                send(i, turn, WANTED.get(mask))
+                send(i, turn, urgency(int(mask)) if mask.isdigit() else None)
             return carry
 
         if r1 - r0 <= 2 and mask in "N":

time: 102 us -> 102 us (level)
  no operation moved by 1% of the time
where the time goes in v4:
time: 102 us
  Pallas kernels  101 us (99%)
    pallas_call x1, Pallas kernels, shards(): pl.pallas_call(kernel, out_shape=(pltpu.VMEM((n, 2, block, rows), jnp.flo...  99.2 us
    pallas_call x1, Pallas kernels, shards(): pl.pallas_call(rescale, out_shape=(out, out), in_specs=[pl.BlockSpec(memo...  2.21 us

profile of v4, /device:TPU:224, one launch (start us, length us, event | category | flops | bytes accessed | tf_op | source)
XLA Modules:
  0.0 102.1 jit_solution(14453587652651753436)
XLA Ops:
  0.6 99.2 %exchange.1 = (f32[64,2,32,256]{3,2,1,0:T(8,128)S(1)}, f32[2,2,32,128]{3,2,1,0:T(8,128)S(1)}) custom-call(f32[256,2048]{1,0:T(8,128)} %first_hbm.1, f32[256,2048]{1,0:T(8,128)} %second_hbm.1), custom_call_target="tpu_custom_call" | custom-call | tf_op jit(solution)/shard_map/exchange/pallas_call | solution.py:255
  99.9 2.2 %rescale.1 = (f32[32,16384]{1,0:T(8,128)}, f32[32,16384]{1,0:T(8,128)}) custom-call(f32[64,2,32,256]{3,2,1,0:T(8,128)S(1)} %get-tuple-element.6.got, f32[2,2,32,128]{3,2,1,0:T(8,128)S(1)} %get-tuple-element.7.total), custom_call_target="tpu_custom_call" | custom-call | tf_op jit(solution)/shard_map/rescale/pallas_call | solution.py:280

commit v5 on v4

--- a/solution.py
+++ b/solution.py
@@ -13,11 +13,13 @@
 PER = 8
 ORDER = (7, 3, 5, 2, 6, 1, 4, 0)
 SHIFT = (1, 0, 1, 0, 1, 0, 0, 0)
-LOADS = (1, 7, 4, 3, 5, 2, 6, 0)
-FIRST = 4
-PHASES = (('F', 0, 4), ('A', 4, 7), ('0', 7, 8), ('1', 7, 8), ('2', 7, 8), ('3', 7, 8), ('4', 7, 8))
+LOADS = (1, 7, 2, 6, 4, 3, 5, 0)
+FIRST = 3
+PHASES = (('G', 0, 2), ('F', 2, 3), ('A', 3, 7), ('0', 7, 8), ('1', 7, 8), ('2', 7, 8), ('3', 7, 8), ('4', 7, 8))
+SECOND = 2
 EARLY = 4
 NEAR = (1, PLANES - 1)
+TWO = (2, PLANES - 2)
 OWN = ORDER.index(0)
 BESIDE = ((1, 2, 3), (3, 1, 2), (2, 3, 1), (1, 3, 2))
 
@@ -117,14 +119,15 @@
         return wanted
 
     def push(mask, r0, r1):
-        which = [i for i in range(PLANES) if not (mask == "N" and ORDER[i] not in NEAR or mask == "F" and ORDER[i] in NEAR)]
+        groups = {"N": NEAR, "T": TWO, "F": [d for d in ORDER if d not in NEAR], "G": [d for d in ORDER if d not in NEAR + TWO]}
+        which = [i for i in range(PLANES) if ORDER[i] in groups.get(mask, ORDER)]
 
         def one(turn, carry):
             for i in which:
                 send(i, turn, urgency(int(mask)) if mask.isdigit() else None)
             return carry
 
-        if r1 - r0 <= 2 and mask in "N":
+        if r1 - r0 <= 2 and mask in "NT":
             for turn in range(r0, r1):
                 one(turn, 0)
         else:
@@ -150,6 +153,7 @@
         transpose(k)
     heard(1, 2)
     hail(2, 2)
+    push("T", 0, SECOND)
     for k in range(6, PLANES):
         transpose(k)
     heard(2, 2)

time: 102 us -> 102 us (level); the launches traced: 102 us -> 100 us
  Pallas kernels: 101 us -> 99.4 us
    pallas_call x1, Pallas kernels: 99.2 us -> 97.2 us  [shards(): pl.pallas_call(kernel, out_shape=(pltpu.VMEM((n, 2, block, rows), jnp.flo...]
where the time goes in v5:
time: 102 us; the launch traced here: 100 us
  Pallas kernels  99.4 us (97%)
    pallas_call x1, Pallas kernels, shards(): pl.pallas_call(kernel, out_shape=(pltpu.VMEM((n, 2, block, rows), jnp.flo...  97.2 us
    pallas_call x1, Pallas kernels, shards(): pl.pallas_call(rescale, out_shape=(out, out), in_specs=[pl.BlockSpec(memo...  2.21 us

profile of v5, /device:TPU:224, one launch (start us, length us, event | category | flops | bytes accessed | tf_op | source)
XLA Modules:
  0.0 100.0 jit_solution(8465917901011150261)
XLA Ops:
  0.6 97.2 %exchange.1 = (f32[64,2,32,256]{3,2,1,0:T(8,128)S(1)}, f32[2,2,32,128]{3,2,1,0:T(8,128)S(1)}) custom-call(f32[256,2048]{1,0:T(8,128)} %first_hbm.1, f32[256,2048]{1,0:T(8,128)} %second_hbm.1), custom_call_target="tpu_custom_call" | custom-call | tf_op jit(solution)/shard_map/exchange/pallas_call | solution.py:259
  97.8 2.2 %rescale.1 = (f32[32,16384]{1,0:T(8,128)}, f32[32,16384]{1,0:T(8,128)}) custom-call(f32[64,2,32,256]{3,2,1,0:T(8,128)S(1)} %get-tuple-element.6.got, f32[2,2,32,128]{3,2,1,0:T(8,128)S(1)} %get-tuple-element.7.total), custom_call_target="tpu_custom_call" | custom-call | tf_op jit(solution)/shard_map/rescale/pallas_call | solution.py:284
